TPU v7x, 32 devices: a whole 2x2x4 slice. The times are simulated.
32 devices in a mesh: gy: 8 (over y, x, core), gx: 4 (over z).
Axes of the slice: x: 2, y: 2, z: 4, core: 2. Of those that a mesh axis runs over, the one named last changes fastest.
Arguments:
- left_factor: bfloat16 [8192, 2048], P('gy', 'gx'), may hold values from -6 to 6
- right_factor: bfloat16 [2048, 8192], P('gy', 'gx'), may hold values from -0.125 to 0.125
Outputs:
- corrected: float32 [8192, 8192], P('gy', 'gx')
All inputs are finite; a program needn't handle non-finite values.
Results may differ from a plain program's by a relative error of at most 0.0003.
Values may be sent and summed in bfloat16 or wider, within the bound.
A program may use at most 192 MiB of HBM per device.

v0:
```python
import jax
import jax.numpy as jnp
from jax import lax
from jax.sharding import PartitionSpec as P


def absorb_panel(left_panel, right_panel):
    return jnp.dot(left_panel, right_panel, preferred_element_type=jnp.float32)


def per_device(left_factor, right_factor):
    right_line = lax.all_gather(right_factor, "gy", axis=0, tiled=True)
    total = absorb_panel(lax.all_gather(left_factor, "gx", axis=1, tiled=True), right_line)
    corrected = total
    row_power = lax.psum(jnp.sum(corrected * corrected, axis=1), "gx")
    corrected = (
        corrected
        * lax.rsqrt(row_power / (corrected.shape[1] * lax.axis_size("gx")) + 1e-06)[:, None]
    )
    return corrected


def solution(mesh):
    placed = (P("gy", "gx"), P("gy", "gx"))
    return jax.shard_map(
        per_device, mesh=mesh, in_specs=placed, out_specs=P("gy", "gx"), check_vma=False
    )
```

profile of v0, /device:TPU:0, one launch (start us, length us, event | category | flops | bytes accessed | tf_op | source)
XLA Modules:
  0.0 187.5 jit_solution(11503262630804149918)
XLA Ops:
  6.5 0.0 all-gather.3.cloned.1.call-start
  6.5 0.7 all-gather.3.cloned.1.call-update
  7.3 0.0 all-gather.5.cloned.1.call-start
  7.3 0.7 all-gather.5.cloned.1.call-update
  8.0 84.4 %all-gather.3.cloned.1.call-done = bf16[1024,2048]{1,0:T(8,128)(2,1)} async-done(((bf16[1024,512]{1,0:T(8,128)(2,1)}), bf16[1024,2048]{1,0:T(8,128)(2,1)}) %all-gather.3.cloned.1.call-update) | async-done | bytes 4194320 | tf_op jit(solution)/shard_map/all_gather | solution.py:13
  92.4 54.7 %all-gather.5.cloned.1.call-done = bf16[2048,2048]{1,0:T(8,128)(2,1)} async-done(((bf16[256,2048]{1,0:T(8,128)(2,1)}), bf16[2048,2048]{1,0:T(8,128)(2,1)}) %all-gather.5.cloned.1.call-update) | async-done | bytes 8388624 | tf_op jit(solution)/shard_map/all_gather | solution.py:12
  147.1 14.5 %multiply_reduce_fusion = (f32[1024]{0:T(1024)S(1)}, f32[1024,2048]{1,0:T(8,128)}) fusion(bf16[1024,2048]{1,0:T(8,128)(2,1)} %all-gather.3.cloned.1.call-done, bf16[2048,2048]{1,0:T(8,128)(2,1)} %all-gather.5.cloned.1.call-done), kind=kOutput, calls=%fused_computation | convolution fusion | flops 8594127872 | bytes 20975616 | tf_op jit(solution)/shard_map/dot_general | solution.py:8
  161.6 11.7 %psum.7 = f32[1024]{0:T(1024)S(1)} all-reduce(f32[1024]{0:T(1024)S(1)} %get-tuple-element.5), channel_id=1, replica_groups=mesh['gy'=8,'gx'=4] {'gx'}, use_global_device_ids=true, to_apply=%region_1.0 | all-reduce | flops 1024 | bytes 8192 | tf_op jit(solution)/shard_map/psum | solution.py:15
  173.3 7.4 %broadcast_multiply_fusion = f32[1024,2048]{1,0:T(8,128)} fusion(f32[1024,2048]{1,0:T(8,128)} %get-tuple-element.6, f32[1024]{0:T(1024)S(1)} %add_rsqrt_fusion), kind=kLoop, calls=%fused_computation.1 | loop fusion | flops 2097152 | bytes 16781312 | tf_op jit(solution)/shard_map/mul | solution.py:17
  (1 shorter events, 0.0 us)
Async XLA Ops:
  6.5 85.9 %all-gather.3.cloned.1.call-start = ((), (), s32[]{:S(2)}) async-start(), calls=%async_computation | async-start | bytes 5242880 | tf_op jit(solution)/shard_map/all_gather | solution.py:13
  7.3 139.8 %all-gather.5.cloned.1.call-start = ((), (), s32[]{:S(2)}) async-start(), calls=%async_computation.1 | async-start | bytes 9437184 | tf_op jit(solution)/shard_map/all_gather | solution.py:12
Sparse Core Ops, SparseCore 0:
  8.9 83.4 all-gather.2
  94.3 52.7 all-gather.4
where the time goes:
time: 188 us
  waiting for transfers between devices  140 us (74%)
  matrix products  14.5 us (8%)
  between operations  13.4 us (7%)
  blocking collectives  11.7 us (6%)
  other arithmetic  7.4 us (4%)
    all_gather x1, waiting for transfers between devices, per_device(): lax.all_gather(left_factor, 'gx', axis=1, tiled=True)  84.4 us
    all_gather x1, waiting for transfers between devices, per_device(): right_line = lax.all_gather(right_factor, 'gy', axis=0, tiled=True)  54.7 us
    dot_general x1, matrix products, absorb_panel(): return jnp.dot(left_panel, right_panel, preferred_element_type=jnp.float32)  14.5 us
    psum x1, blocking collectives, per_device(): row_power = lax.psum(jnp.sum(corrected * corrected, axis=1), 'gx')  11.7 us
    mul x1, other arithmetic, per_device(): corrected * lax.rsqrt(row_power / (corrected.shape[1] * lax.axis_size('gx...  7.39 us
  transfers between devices with their start and end apart: 2, of which 2 were waited for; matrix products, arithmetic and copies ran while one was open for 0% of the time, Pallas kernels for 0%

commit v1 on v0

--- a/solution.py
+++ b/solution.py
@@ -10,7 +10,7 @@
 
 def per_device(left_factor, right_factor):
     right_line = lax.all_gather(right_factor, "gy", axis=0, tiled=True)
-    total = absorb_panel(lax.all_gather(left_factor, "gx", axis=1, tiled=True), right_line)
+    total = absorb_panel(jnp.concatenate(lax.all_gather(left_factor, "gx"), axis=1), right_line)
     corrected = total
     row_power = lax.psum(jnp.sum(corrected * corrected, axis=1), "gx")
     corrected = (

time: 188 us -> 188 us (level)
  local copies, waits for them, and re-layouts: 0 us -> 6.25 us
  waiting for transfers between devices: 140 us -> 134 us
    all_gather x1, waiting for transfers between devices: 54.7 us -> 48.4 us  [per_device(): right_line = lax.all_gather(right_factor, 'gy', axis=0, tiled=True)]
    reshape x0 -> x1, local copies, waits for them, and re-layouts: none -> 6.25 us  [per_device(): jnp.concatenate(lax.all_gather(left_factor, 'gx'), axis=1)]
  transfers between devices with their start and end apart: 2 -> 2, of which waited for: 2 -> 2; matrix products, arithmetic and copies ran while one was open for 0% -> 3% of each run, Pallas kernels for 0% -> 0%
where the time goes in v1:
time: 188 us
  waiting for transfers between devices  134 us (71%)
  matrix products  14.7 us (8%)
  between operations  13.4 us (7%)
  blocking collectives  11.7 us (6%)
  other arithmetic  7.4 us (4%)
  local copies, waits for them, and re-layouts  6.25 us (3%)
    all_gather x1, waiting for transfers between devices, per_device(): lax.all_gather(left_factor, 'gx')  84.4 us
    all_gather x1, waiting for transfers between devices, per_device(): right_line = lax.all_gather(right_factor, 'gy', axis=0, tiled=True)  48.4 us
    dot_general x1, matrix products, absorb_panel(): return jnp.dot(left_panel, right_panel, preferred_element_type=jnp.float32)  14.7 us
    psum x1, blocking collectives, per_device(): row_power = lax.psum(jnp.sum(corrected * corrected, axis=1), 'gx')  11.7 us
    mul x1, other arithmetic, per_device(): corrected * lax.rsqrt(row_power / (corrected.shape[1] * lax.axis_size('gx...  7.39 us
    reshape x1, local copies, waits for them, and re-layouts, per_device(): jnp.concatenate(lax.all_gather(left_factor, 'gx'), axis=1)  6.25 us
  transfers between devices with their start and end apart: 2, of which 2 were waited for; matrix products, arithmetic and copies ran while one was open for 3% of the time, Pallas kernels for 0%

profile of v1, /device:TPU:0, one launch (start us, length us, event | category | flops | bytes accessed | tf_op | source)
XLA Modules:
  0.0 187.7 jit_solution(5825700000848456008)
XLA Ops:
  6.5 0.0 all-gather.6.cloned.1.call-start
  6.5 0.7 all-gather.6.cloned.1.call-update
  7.3 0.0 all-gather.4.cloned.1.call-start
  7.3 0.7 all-gather.4.cloned.1.call-update
  8.0 84.4 %all-gather.6.cloned.1.call-done = bf16[4096,512]{1,0:T(8,128)(2,1)} async-done(((bf16[1024,512]{1,0:T(8,128)(2,1)}), bf16[4096,512]{1,0:T(8,128)(2,1)}) %all-gather.6.cloned.1.call-update) | async-done | bytes 4194320 | tf_op jit(solution)/shard_map/all_gather | solution.py:13
  92.4 6.2 %copy.3 = bf16[1024,4,512]{0,2,1:T(8,128)(2,1)} copy(bf16[1024,4,512]{2,0,1:T(8,128)(2,1)} %bitcast.6) | data formatting | bytes 8388608 | tf_op jit(solution)/shard_map/reshape | solution.py:13
  98.6 48.4 %all-gather.4.cloned.1.call-done = bf16[2048,2048]{1,0:T(8,128)(2,1)} async-done(((bf16[256,2048]{1,0:T(8,128)(2,1)}), bf16[2048,2048]{1,0:T(8,128)(2,1)}) %all-gather.4.cloned.1.call-update) | async-done | bytes 8388624 | tf_op jit(solution)/shard_map/all_gather | solution.py:12
  147.1 14.7 %multiply_reduce_fusion = (f32[1024]{0:T(1024)S(1)}, f32[1024,2048]{1,0:T(8,128)}) fusion(bf16[1024,2048]{0,1:T(8,128)(2,1)} %bitcast.7, bf16[2048,2048]{1,0:T(8,128)(2,1)} %all-gather.4.cloned.1.call-done), kind=kOutput, calls=%fused_computation | convolution fusion | flops 8594127872 | bytes 20975616 | tf_op jit(solution)/shard_map/dot_general | solution.py:8
  161.8 11.7 %psum.7 = f32[1024]{0:T(1024)S(1)} all-reduce(f32[1024]{0:T(1024)S(1)} %get-tuple-element.5), channel_id=1, replica_groups=mesh['gy'=8,'gx'=4] {'gx'}, use_global_device_ids=true, to_apply=%region_1.0 | all-reduce | flops 1024 | bytes 8192 | tf_op jit(solution)/shard_map/psum | solution.py:15
  173.4 7.4 %broadcast_multiply_fusion = f32[1024,2048]{1,0:T(8,128)} fusion(f32[1024,2048]{1,0:T(8,128)} %get-tuple-element.6, f32[1024]{0:T(1024)S(1)} %add_rsqrt_fusion), kind=kLoop, calls=%fused_computation.1 | loop fusion | flops 2097152 | bytes 16781312 | tf_op jit(solution)/shard_map/mul | solution.py:17
  (1 shorter events, 0.0 us)
Async XLA Ops:
  6.5 85.9 %all-gather.6.cloned.1.call-start = ((), (), s32[]{:S(2)}) async-start(), calls=%async_computation.1 | async-start | bytes 5242880 | tf_op jit(solution)/shard_map/all_gather | solution.py:13
  7.3 139.8 %all-gather.4.cloned.1.call-start = ((), (), s32[]{:S(2)}) async-start(), calls=%async_computation | async-start | bytes 9437184 | tf_op jit(solution)/shard_map/all_gather | solution.py:12
Sparse Core Ops, SparseCore 0:
  8.9 83.4 all-gather.5
  94.3 52.7 all-gather.3

commit v2 on v0

--- a/solution.py
+++ b/solution.py
@@ -12,7 +12,7 @@
     right_line = lax.all_gather(right_factor, "gy", axis=0, tiled=True)
     total = absorb_panel(lax.all_gather(left_factor, "gx", axis=1, tiled=True), right_line)
     corrected = total
-    row_power = lax.psum(jnp.sum(corrected * corrected, axis=1), "gx")
+    row_power = jnp.sum(lax.all_gather(jnp.sum(corrected * corrected, axis=1), "gx"), axis=0)
     corrected = (
         corrected
         * lax.rsqrt(row_power / (corrected.shape[1] * lax.axis_size("gx")) + 1e-06)[:, None]

time: 188 us -> 189 us (level)
    all_gather x0 -> x1, blocking collectives: none -> 13.2 us  [per_device(): lax.all_gather(jnp.sum(corrected * corrected, axis=1), 'gx')]
    psum x1 -> x0, blocking collectives: 11.7 us -> none  [per_device(): row_power = lax.psum(jnp.sum(corrected * corrected, axis=1), 'gx')]
where the time goes in v2:
time: 189 us
  waiting for transfers between devices  140 us (74%)
  matrix products  14.5 us (8%)
  between operations  13.4 us (7%)
  blocking collectives  13.2 us (7%)
  other arithmetic  7.41 us (4%)
    all_gather x1, waiting for transfers between devices, per_device(): lax.all_gather(left_factor, 'gx', axis=1, tiled=True)  84.4 us
    all_gather x1, waiting for transfers between devices, per_device(): right_line = lax.all_gather(right_factor, 'gy', axis=0, tiled=True)  54.7 us
    dot_general x1, matrix products, absorb_panel(): return jnp.dot(left_panel, right_panel, preferred_element_type=jnp.float32)  14.5 us
    all_gather x1, blocking collectives, per_device(): lax.all_gather(jnp.sum(corrected * corrected, axis=1), 'gx')  13.2 us
    mul x1, other arithmetic, per_device(): corrected * lax.rsqrt(row_power / (corrected.shape[1] * lax.axis_size('gx...  7.39 us
  transfers between devices with their start and end apart: 2, of which 2 were waited for; matrix products, arithmetic and copies ran while one was open for 0% of the time, Pallas kernels for 0%

profile of v2, /device:TPU:0, one launch (start us, length us, event | category | flops | bytes accessed | tf_op | source)
XLA Modules:
  0.0 189.1 jit_solution(4096460527689829625)
XLA Ops:
  6.5 0.0 all-gather.4.cloned.1.call-start
  6.5 0.7 all-gather.4.cloned.1.call-update
  7.3 0.0 all-gather.6.cloned.1.call-start
  7.3 0.7 all-gather.6.cloned.1.call-update
  8.0 84.4 %all-gather.4.cloned.1.call-done = bf16[1024,2048]{1,0:T(8,128)(2,1)} async-done(((bf16[1024,512]{1,0:T(8,128)(2,1)}), bf16[1024,2048]{1,0:T(8,128)(2,1)}) %all-gather.4.cloned.1.call-update) | async-done | bytes 4194320 | tf_op jit(solution)/shard_map/all_gather | solution.py:13
  92.4 54.7 %all-gather.6.cloned.1.call-done = bf16[2048,2048]{1,0:T(8,128)(2,1)} async-done(((bf16[256,2048]{1,0:T(8,128)(2,1)}), bf16[2048,2048]{1,0:T(8,128)(2,1)}) %all-gather.6.cloned.1.call-update) | async-done | bytes 8388624 | tf_op jit(solution)/shard_map/all_gather | solution.py:12
  147.1 14.5 %multiply_reduce_fusion = (f32[1024]{0:T(1024)S(1)}, f32[1024,2048]{1,0:T(8,128)}) fusion(bf16[1024,2048]{1,0:T(8,128)(2,1)} %all-gather.4.cloned.1.call-done, bf16[2048,2048]{1,0:T(8,128)(2,1)} %all-gather.6.cloned.1.call-done), kind=kOutput, calls=%fused_computation | convolution fusion | flops 8594127872 | bytes 20975616 | tf_op jit(solution)/shard_map/dot_general | solution.py:8
  161.6 13.2 %all-gather = f32[4096]{0:T(1024)S(1)} all-gather(f32[1024]{0:T(1024)S(1)} %get-tuple-element.5), channel_id=2, replica_groups=mesh['gy'=8,'gx'=4] {'gx'}, dimensions={0}, use_global_device_ids=true | all-gather | bytes 20480 | tf_op jit(solution)/shard_map/all_gather | solution.py:15
  174.9 7.4 %broadcast_multiply_fusion = f32[1024,2048]{1,0:T(8,128)} fusion(f32[1024,2048]{1,0:T(8,128)} %get-tuple-element.6, f32[1024]{0:T(1024)S(1)} %add_rsqrt_fusion), kind=kLoop, calls=%fused_computation.1 | loop fusion | flops 2097152 | bytes 16781312 | tf_op jit(solution)/shard_map/mul | solution.py:17
  (3 shorter events, 0.0 us)
Async XLA Ops:
  6.5 85.9 %all-gather.4.cloned.1.call-start = ((), (), s32[]{:S(2)}) async-start(), calls=%async_computation | async-start | bytes 5242880 | tf_op jit(solution)/shard_map/all_gather | solution.py:13
  7.3 139.8 %all-gather.6.cloned.1.call-start = ((), (), s32[]{:S(2)}) async-start(), calls=%async_computation.1 | async-start | bytes 9437184 | tf_op jit(solution)/shard_map/all_gather | solution.py:12
Sparse Core Ops, SparseCore 0:
  8.9 83.4 all-gather.3
  94.3 52.7 all-gather.5
